TPU v7x, 128 devices: a whole 4x4x4 slice. The times are simulated.
128 devices in a mesh: outer: 8 (over x, z_hi), inner: 16 (over z_lo, y, core).
Axes of the slice: x: 4, y: 4, z: 4 (z_hi: 2, z_lo: 2; z = z_hi * 2 + z_lo), core: 2. Of those that a mesh axis runs over, the one named last changes fastest.
Arguments:
- queries: bfloat16 [16384, 4096], P(('outer', 'inner')), may hold values from -24 to 24, as said below
- keys: bfloat16 [16384, 1024], P(('outer', 'inner')), may hold values from -24 to 24, as said below
- values: bfloat16 [16384, 1024], P(('outer', 'inner')), may hold values from -6 to 6
Outputs:
- attended: bfloat16 [16384, 4096], P(('outer', 'inner'))
Inputs may be any that keep to these rules, and one draw needn't show every extreme that they name: `queries`: entries of order one, a few larger. `keys`: entries of order one, a few larger.
All inputs are finite; a program needn't handle non-finite values.
Results may differ from a plain program's by a relative error of at most 0.008.
Values may be sent and summed in bfloat16 or wider, within the bound.
A program may use at most 128 MiB of HBM per device.

v0:
```python
import jax
import jax.numpy as jnp
from jax import lax
from jax.sharding import Mesh
from jax.sharding import PartitionSpec as P

QH = 32
KVH = 8
HD = 128
INNER = ("inner_0", "inner_1", "inner_2")
OUTER_INNER = ("outer", "inner_0", "inner_1", "inner_2")


def sent_together(arrays, axis, split_dim, concat_dim, along):
    widths = [a.shape[along] for a in arrays]
    both = jnp.concatenate(arrays, axis=along)
    result = lax.all_to_all(both, axis, split_axis=split_dim, concat_axis=concat_dim, tiled=True)
    return tuple(jnp.split(result, [sum(widths[:k]) for k in range(1, len(widths))], axis=along))


def shifted(block, axis, distance):
    devices = range(lax.axis_size(axis))
    route = [(i - distance, i) for i in devices if i - distance in devices]
    return lax.ppermute(block, axis, route)


def in_blocks(shard, dim, count):
    before, after = (shard.shape[:dim], shard.shape[dim + 1 :])
    return jnp.moveaxis(shard.reshape(*before, count, -1, *after), dim, 0)


def joined_along(parts, dim):
    lengths = list(parts.shape[1:])
    lengths[dim] *= parts.shape[0]
    return jnp.moveaxis(parts, 0, dim).reshape(lengths)


def exchange_in_order(parts, axes, sequence):
    lengths = [lax.axis_size(a) for a in axes]
    parts = parts.reshape(*lengths, *parts.shape[1:])
    for k in sequence:
        parts = lax.all_to_all(parts, axes[k], split_axis=k, concat_axis=k, tiled=True)
    return parts.reshape(-1, *parts.shape[len(axes) :])


def core_and_chips(shard, groups, sequence, split_dim, concat_dim):
    count = lax.axis_size(groups[0]) * lax.axis_size(groups[1])
    parts = in_blocks(shard, split_dim, count)
    return joined_along(exchange_in_order(parts, groups, sequence), concat_dim)


def attend(state, near_keys, near_values, allowed, grouped):
    rows = near_keys.shape[0]
    heads = near_keys.shape[1]
    size = 256
    count = rows // size
    scale = 1.0 / HD**0.5
    key_blocks = near_keys.reshape(count, size, heads, HD)
    value_blocks = near_values.reshape(count, size, heads, HD)

    def one_block(carry, pieces):
        peak, total, accum = carry
        key_block, value_block = pieces
        scores = (
            jnp.einsum("qgrd,kgd->grqk", grouped, key_block, preferred_element_type=jnp.float32)
            * scale
        )
        scores = jnp.where(allowed, scores, -jnp.inf)
        upper = jnp.maximum(peak, jnp.max(scores, axis=-1))
        factor = jnp.exp(peak - upper)
        weights = jnp.exp(scores - upper[..., None])
        total = total * factor + jnp.sum(weights, axis=-1)
        update = jnp.einsum(
            "grqk,kgd->grqd",
            weights.astype(jnp.bfloat16),
            value_block,
            preferred_element_type=jnp.float32,
        )
        accum = accum * factor[..., None] + update
        return ((upper, total, accum), None)

    state, unused = lax.scan(one_block, state, (key_blocks, value_blocks))
    return state


def fresh_state(heads, ratio, tokens):
    return (
        jnp.full((heads, ratio, tokens), -jnp.inf, jnp.float32),
        jnp.zeros((heads, ratio, tokens), jnp.float32),
        jnp.zeros((heads, ratio, tokens, HD), jnp.float32),
    )


def shards(queries, keys, values):
    tokens = queries.shape[0]
    position = lax.axis_index("outer")
    before_ok = position > 0
    after_ok = position < lax.axis_size("outer") - 1
    members = lax.axis_size(INNER)
    per_device = QH // members
    repeat = members // KVH
    query_heads = queries.reshape(tokens, QH, HD)
    key_heads = jnp.repeat(keys.reshape(tokens, KVH, HD), repeat, axis=1)
    value_heads = jnp.repeat(values.reshape(tokens, KVH, HD), repeat, axis=1)
    group_q, group_k, group_v = (
        lax.all_to_all(query_heads, INNER, split_axis=1, concat_axis=0, tiled=True),
        *sent_together((key_heads, value_heads), INNER, 1, 0, 2),
    )
    rows = group_q.shape[0]
    grouped = group_q.reshape(rows, 1, per_device, HD)
    state = attend(fresh_state(1, per_device, rows), group_k, group_v, True, grouped)
    early_k, early_v = shifted((group_k, group_v), "outer", 1)
    state = attend(state, early_k, early_v, before_ok, grouped)
    late_k, late_v = shifted((group_k, group_v), "outer", -1)
    state = attend(state, late_k, late_v, after_ok, grouped)
    peak, total, accum = state
    mixed = (accum / total[..., None]).astype(jnp.bfloat16)
    mixed = mixed.reshape(per_device, rows, HD).transpose(1, 0, 2)
    back = core_and_chips(mixed, (("inner_0", "inner_1"), "inner_2"), (1, 0), 0, 1)
    return back.reshape(tokens, QH * HD)


def solution(mesh):
    torus = Mesh(
        mesh.devices.reshape(mesh.shape["outer"], 2, 4, 2),
        ("outer", "inner_0", "inner_1", "inner_2"),
    )
    in_specs = (P(OUTER_INNER, None), P(OUTER_INNER, None), P(OUTER_INNER, None))
    out_specs = P(OUTER_INNER, None)
    return jax.shard_map(
        shards, mesh=torus, in_specs=in_specs, out_specs=out_specs, check_vma=False
    )
```

profile of v0, /device:TPU:1, one launch (start us, length us, event | category | flops | bytes accessed | tf_op | source)
XLA Modules:
  0.0 243.5 jit_solution(4281796568999556931)
XLA Ops:
  3.4 7.3 %all-to-all-start = ((bf16[128,16,256]{2,0,1:T(8,128)(2,1)}), bf16[128,16,256]{2,0,1:T(8,128)(2,1)S(1)}, u32[]{:S(2)}, u32[]{:S(2)}) async-start(bf16[128,16,256]{2,0,1:T(8,128)(2,1)} %pad_maximum_fusion), calls=%async_computation | async-start | bytes 2097152 | tf_op jit(solution)/shard_map/all_to_all | solution.py:17
  12.1 14.4 %all-to-all-done = bf16[128,16,256]{2,0,1:T(8,128)(2,1)S(1)} async-done(((bf16[128,16,256]{2,0,1:T(8,128)(2,1)}), bf16[128,16,256]{2,0,1:T(8,128)(2,1)S(1)}, u32[]{:S(2)}, u32[]{:S(2)}) %all-to-all-start) | async-done | bytes 1048608 | tf_op jit(solution)/shard_map/all_to_all | solution.py:17
  27.5 4.2 %all-to-all-start.1 = ((bf16[128,32,128]{0,2,1:T(8,128)(2,1)}), bf16[128,32,128]{0,2,1:T(8,128)(2,1)S(1)}, u32[]{:S(2)}, u32[]{:S(2)}) async-start(bf16[128,32,128]{0,2,1:T(8,128)(2,1)} %bitcast.34), calls=%async_computation.1 | async-start | bytes 2097152 | tf_op jit(solution)/shard_map/all_to_all | solution.py:106
  34.0 6.0 %collective-permute-start = (bf16[2048,1,128]{2,0,1:T(8,128)(2,1)}, bf16[2048,1,128]{2,0,1:T(8,128)(2,1)}, u32[]{:S(2)}, u32[]{:S(2)}) collective-permute-start(bf16[2048,1,128]{2,0,1:T(8,128)(2,1)} %get-tuple-element.222), channel_id=1, source_target_pairs={{0,16},{16,32},{32,48},{48,64},{64,80},{80,96},{96,112},{1,17},{17... | collective-permute-start | bytes 1572872 | tf_op jit(solution)/shard_map/ppermute | solution.py:24
  41.3 6.3 %collective-permute-start.1 = (bf16[2048,1,128]{2,0,1:T(8,128)(2,1)}, bf16[2048,1,128]{2,0,1:T(8,128)(2,1)}, u32[]{:S(2)}, u32[]{:S(2)}) collective-permute-start(bf16[2048,1,128]{2,0,1:T(8,128)(2,1)} %get-tuple-element.221), channel_id=1, source_target_pairs={{0,16},{16,32},{32,48},{48,64},{64,80},{80,96},{96,112},{1,17},{17... | collective-permute-start | bytes 1572872 | tf_op jit(solution)/shard_map/ppermute | solution.py:24
  51.5 62.2 %while.45 = (s32[]{:T(128)}, f32[1,2,2048]{2,1,0:T(2,128)S(1)}, f32[1,2,2048]{2,1,0:T(2,128)S(1)}, f32[1,2,2048,128]{3,2,1,0:T(8,128)S(1)}, bf16[8,256,1,128]{3,...) while((s32[]{:T(128)}, f32[1,2,2048]{2,1,0:T(2,128)S(1)}, ...), condition=%wide.region_3.4_spmd.clone, body=%wide.region_0.3_spmd.clone.sunk | while | flops 546856960 | bytes 34997380 | solution.py:82
  51.5 3.5 %bitcast_reduce_fusion.8 = (f32[2,2048]{1,0:T(2,128)S(1)}, f32[256,2048,2]{1,0,2:T(8,128)}) fusion(bf16[2048,1,2,128]{3,0,2,1:T(8,128)(2,1)S(1)} %get-tuple-element.411, bf16[8,256,1,128]{3,1,2,0:T(8,128)(2,1)} %get-tuple-element.410, s32[]{:T(128)} %get-tuple-element.397), kind=kOutput, calls=%fused_computation.55.clone.1 | convolution fusion | flops 270528512 | bytes 5325312 | tf_op jit(solution)/shard_map/while/body/eval_jaxpr/qgrd,kgd->grqk/dot_general | solution.py:65
  59.3 3.5 %bitcast_reduce_fusion.8 = (f32[2,2048]{1,0:T(2,128)S(1)}, f32[256,2048,2]{1,0,2:T(8,128)}) fusion(bf16[2048,1,2,128]{3,0,2,1:T(8,128)(2,1)S(1)} %get-tuple-element.411, bf16[8,256,1,128]{3,1,2,0:T(8,128)(2,1)} %get-tuple-element.410, s32[]{:T(128)} %get-tuple-element.397), kind=kOutput, calls=%fused_computation.55.clone.1 | convolution fusion | flops 270528512 | bytes 5325312 | tf_op jit(solution)/shard_map/while/body/eval_jaxpr/qgrd,kgd->grqk/dot_general | solution.py:65
  62.8 3.3 %fusion.92 = f32[1,2,2048,128]{3,2,1,0:T(8,128)S(1)} fusion(f32[256,2048,2]{1,0,2:T(8,128)} %get-tuple-element.386, f32[1,2,2048,128]{3,2,1,0:T(8,128)S(1)} %get-tuple-element.400, f32[2,2048]{1,0:T(2,128)S(1)} %bitcast.243, f32[2,2048]{1,0:T(2,128)S(1)} %get-tuple-element.387, pred[]{:T(512)S(6)} %compare.3, ...), kind=kOutput, calls=%fused_computation.60.clone.1 | convolution fusion | flops 273154048 | bytes 8487425 | tf_op jit(solution)/shard_map/while/body/eval_jaxpr/grqk,kgd->grqd/dot_general | solution.py:73
  67.1 3.5 %bitcast_reduce_fusion.8 = (f32[2,2048]{1,0:T(2,128)S(1)}, f32[256,2048,2]{1,0,2:T(8,128)}) fusion(bf16[2048,1,2,128]{3,0,2,1:T(8,128)(2,1)S(1)} %get-tuple-element.411, bf16[8,256,1,128]{3,1,2,0:T(8,128)(2,1)} %get-tuple-element.410, s32[]{:T(128)} %get-tuple-element.397), kind=kOutput, calls=%fused_computation.55.clone.1 | convolution fusion | flops 270528512 | bytes 5325312 | tf_op jit(solution)/shard_map/while/body/eval_jaxpr/qgrd,kgd->grqk/dot_general | solution.py:65
  70.6 3.3 %fusion.92 = f32[1,2,2048,128]{3,2,1,0:T(8,128)S(1)} fusion(f32[256,2048,2]{1,0,2:T(8,128)} %get-tuple-element.386, f32[1,2,2048,128]{3,2,1,0:T(8,128)S(1)} %get-tuple-element.400, f32[2,2048]{1,0:T(2,128)S(1)} %bitcast.243, f32[2,2048]{1,0:T(2,128)S(1)} %get-tuple-element.387, pred[]{:T(512)S(6)} %compare.3, ...), kind=kOutput, calls=%fused_computation.60.clone.1 | convolution fusion | flops 273154048 | bytes 8487425 | tf_op jit(solution)/shard_map/while/body/eval_jaxpr/grqk,kgd->grqd/dot_general | solution.py:73
  74.8 3.5 %bitcast_reduce_fusion.8 = (f32[2,2048]{1,0:T(2,128)S(1)}, f32[256,2048,2]{1,0,2:T(8,128)}) fusion(bf16[2048,1,2,128]{3,0,2,1:T(8,128)(2,1)S(1)} %get-tuple-element.411, bf16[8,256,1,128]{3,1,2,0:T(8,128)(2,1)} %get-tuple-element.410, s32[]{:T(128)} %get-tuple-element.397), kind=kOutput, calls=%fused_computation.55.clone.1 | convolution fusion | flops 270528512 | bytes 5325312 | tf_op jit(solution)/shard_map/while/body/eval_jaxpr/qgrd,kgd->grqk/dot_general | solution.py:65
  78.4 3.3 %fusion.92 = f32[1,2,2048,128]{3,2,1,0:T(8,128)S(1)} fusion(f32[256,2048,2]{1,0,2:T(8,128)} %get-tuple-element.386, f32[1,2,2048,128]{3,2,1,0:T(8,128)S(1)} %get-tuple-element.400, f32[2,2048]{1,0:T(2,128)S(1)} %bitcast.243, f32[2,2048]{1,0:T(2,128)S(1)} %get-tuple-element.387, pred[]{:T(512)S(6)} %compare.3, ...), kind=kOutput, calls=%fused_computation.60.clone.1 | convolution fusion | flops 273154048 | bytes 8487425 | tf_op jit(solution)/shard_map/while/body/eval_jaxpr/grqk,kgd->grqd/dot_general | solution.py:73
  82.6 3.5 %bitcast_reduce_fusion.8 = (f32[2,2048]{1,0:T(2,128)S(1)}, f32[256,2048,2]{1,0,2:T(8,128)}) fusion(bf16[2048,1,2,128]{3,0,2,1:T(8,128)(2,1)S(1)} %get-tuple-element.411, bf16[8,256,1,128]{3,1,2,0:T(8,128)(2,1)} %get-tuple-element.410, s32[]{:T(128)} %get-tuple-element.397), kind=kOutput, calls=%fused_computation.55.clone.1 | convolution fusion | flops 270528512 | bytes 5325312 | tf_op jit(solution)/shard_map/while/body/eval_jaxpr/qgrd,kgd->grqk/dot_general | solution.py:65
  86.1 3.3 %fusion.92 = f32[1,2,2048,128]{3,2,1,0:T(8,128)S(1)} fusion(f32[256,2048,2]{1,0,2:T(8,128)} %get-tuple-element.386, f32[1,2,2048,128]{3,2,1,0:T(8,128)S(1)} %get-tuple-element.400, f32[2,2048]{1,0:T(2,128)S(1)} %bitcast.243, f32[2,2048]{1,0:T(2,128)S(1)} %get-tuple-element.387, pred[]{:T(512)S(6)} %compare.3, ...), kind=kOutput, calls=%fused_computation.60.clone.1 | convolution fusion | flops 273154048 | bytes 8487425 | tf_op jit(solution)/shard_map/while/body/eval_jaxpr/grqk,kgd->grqd/dot_general | solution.py:73
  90.4 3.5 %bitcast_reduce_fusion.8 = (f32[2,2048]{1,0:T(2,128)S(1)}, f32[256,2048,2]{1,0,2:T(8,128)}) fusion(bf16[2048,1,2,128]{3,0,2,1:T(8,128)(2,1)S(1)} %get-tuple-element.411, bf16[8,256,1,128]{3,1,2,0:T(8,128)(2,1)} %get-tuple-element.410, s32[]{:T(128)} %get-tuple-element.397), kind=kOutput, calls=%fused_computation.55.clone.1 | convolution fusion | flops 270528512 | bytes 5325312 | tf_op jit(solution)/shard_map/while/body/eval_jaxpr/qgrd,kgd->grqk/dot_general | solution.py:65
  98.2 3.5 %bitcast_reduce_fusion.8 = (f32[2,2048]{1,0:T(2,128)S(1)}, f32[256,2048,2]{1,0,2:T(8,128)}) fusion(bf16[2048,1,2,128]{3,0,2,1:T(8,128)(2,1)S(1)} %get-tuple-element.411, bf16[8,256,1,128]{3,1,2,0:T(8,128)(2,1)} %get-tuple-element.410, s32[]{:T(128)} %get-tuple-element.397), kind=kOutput, calls=%fused_computation.55.clone.1 | convolution fusion | flops 270528512 | bytes 5325312 | tf_op jit(solution)/shard_map/while/body/eval_jaxpr/qgrd,kgd->grqk/dot_general | solution.py:65
  101.7 3.3 %fusion.92 = f32[1,2,2048,128]{3,2,1,0:T(8,128)S(1)} fusion(f32[256,2048,2]{1,0,2:T(8,128)} %get-tuple-element.386, f32[1,2,2048,128]{3,2,1,0:T(8,128)S(1)} %get-tuple-element.400, f32[2,2048]{1,0:T(2,128)S(1)} %bitcast.243, f32[2,2048]{1,0:T(2,128)S(1)} %get-tuple-element.387, pred[]{:T(512)S(6)} %compare.3, ...), kind=kOutput, calls=%fused_computation.60.clone.1 | convolution fusion | flops 273154048 | bytes 8487425 | tf_op jit(solution)/shard_map/while/body/eval_jaxpr/grqk,kgd->grqd/dot_general | solution.py:73
  105.9 3.5 %bitcast_reduce_fusion.8 = (f32[2,2048]{1,0:T(2,128)S(1)}, f32[256,2048,2]{1,0,2:T(8,128)}) fusion(bf16[2048,1,2,128]{3,0,2,1:T(8,128)(2,1)S(1)} %get-tuple-element.411, bf16[8,256,1,128]{3,1,2,0:T(8,128)(2,1)} %get-tuple-element.410, s32[]{:T(128)} %get-tuple-element.397), kind=kOutput, calls=%fused_computation.55.clone.1 | convolution fusion | flops 270528512 | bytes 5325312 | tf_op jit(solution)/shard_map/while/body/eval_jaxpr/qgrd,kgd->grqk/dot_general | solution.py:65
  109.5 3.3 %fusion.92 = f32[1,2,2048,128]{3,2,1,0:T(8,128)S(1)} fusion(f32[256,2048,2]{1,0,2:T(8,128)} %get-tuple-element.386, f32[1,2,2048,128]{3,2,1,0:T(8,128)S(1)} %get-tuple-element.400, f32[2,2048]{1,0:T(2,128)S(1)} %bitcast.243, f32[2,2048]{1,0:T(2,128)S(1)} %get-tuple-element.387, pred[]{:T(512)S(6)} %compare.3, ...), kind=kOutput, calls=%fused_computation.60.clone.1 | convolution fusion | flops 273154048 | bytes 8487425 | tf_op jit(solution)/shard_map/while/body/eval_jaxpr/grqk,kgd->grqd/dot_general | solution.py:73
  113.7 41.8 %while.43 = (s32[]{:T(128)}, f32[1,2,2048]{2,1,0:T(2,128)S(1)}, f32[1,2,2048]{2,1,0:T(2,128)S(1)}, f32[1,2,2048,128]{3,2,1,0:T(8,128)S(1)}, pred[]{:T(512)}, /*i...) while((s32[]{:T(128)}, f32[1,2,2048]{2,1,0:T(2,128)S(1)}, ...), condition=%wide.region_7.8_spmd, body=%wide.region_4.7_spmd.sunk | while | flops 549466112 | bytes 18221148 | solution.py:82
  155.5 41.8 %while.44 = (s32[]{:T(128)}, f32[1,2,2048]{2,1,0:T(2,128)S(1)}, f32[1,2,2048]{2,1,0:T(2,128)S(1)}, f32[1,2,2048,128]{3,2,1,0:T(8,128)S(1)}, pred[]{:T(512)}, /*i...) while((s32[]{:T(128)}, f32[1,2,2048]{2,1,0:T(2,128)S(1)}, ...), condition=%wide.region_11.12_spmd, body=%wide.region_8.11_spmd.sunk | while | flops 549466112 | bytes 18221148 | solution.py:82
  198.1 5.3 %all_to_all.43 = bf16[8,2,128,2,128]{4,2,0,3,1:T(8,128)(2,1)S(1)} all-to-all(bf16[8,2,128,2,128]{4,2,0,3,1:T(8,128)(2,1)S(1)} %copy.53), channel_id=1, replica_groups=mesh['outer'=8,'inner_0'=2,'inner_1'=4,'inner_2'=2] {'inner_2'}, dimensions={1} | all-to-all | bytes 2097152 | tf_op jit(solution)/shard_map/all_to_all | solution.py:42
  203.5 38.0 %all_to_all.44 = bf16[8,2,128,2,128]{4,2,1,3,0:T(8,128)(2,1)S(1)} all-to-all(bf16[8,2,128,2,128]{4,2,1,3,0:T(8,128)(2,1)S(1)} %copy.54), channel_id=1, replica_groups=mesh['outer'=8,'inner_0'=2,'inner_1'=4,'inner_2'=2] {'inner_0','inner_1'}, dimensions={0} | all-to-all | bytes 2097152 | tf_op jit(solution)/shard_map/all_to_all | solution.py:42
  (178 shorter events, 113.1 us)
Async XLA Ops:
  0.0 1.0 copy-start
  1.0 9.8 %copy-start.4 = (bf16[128,4096]{1,0:T(8,128)(2,1)S(1)}, bf16[128,4096]{1,0:T(8,128)(2,1)}, u32[]{:S(2)}) copy-start(bf16[128,4096]{1,0:T(8,128)(2,1)} %param.9) | copy-start | bytes 3145732
  3.4 23.1 %all-to-all-start = ((bf16[128,16,256]{2,0,1:T(8,128)(2,1)}), bf16[128,16,256]{2,0,1:T(8,128)(2,1)S(1)}, u32[]{:S(2)}, u32[]{:S(2)}) async-start(bf16[128,16,256]{2,0,1:T(8,128)(2,1)} %pad_maximum_fusion), calls=%async_computation | async-start | bytes 2097152 | tf_op jit(solution)/shard_map/all_to_all | solution.py:17
  26.5 1.0 copy-start.3
  27.5 21.4 %all-to-all-start.1 = ((bf16[128,32,128]{0,2,1:T(8,128)(2,1)}), bf16[128,32,128]{0,2,1:T(8,128)(2,1)S(1)}, u32[]{:S(2)}, u32[]{:S(2)}) async-start(bf16[128,32,128]{0,2,1:T(8,128)(2,1)} %bitcast.34), calls=%async_computation.1 | async-start | bytes 2097152 | tf_op jit(solution)/shard_map/all_to_all | solution.py:106
  34.0 79.7 %collective-permute-start = (bf16[2048,1,128]{2,0,1:T(8,128)(2,1)}, bf16[2048,1,128]{2,0,1:T(8,128)(2,1)}, u32[]{:S(2)}, u32[]{:S(2)}) collective-permute-start(bf16[2048,1,128]{2,0,1:T(8,128)(2,1)} %get-tuple-element.222), channel_id=1, source_target_pairs={{0,16},{16,32},{32,48},{48,64},{64,80},{80,96},{96,112},{1,17},{17... | collective-permute-start | bytes 1572872 | tf_op jit(solution)/shard_map/ppermute | solution.py:24
  40.0 115.5 %collective-permute-start.2 = (bf16[2048,1,128]{2,0,1:T(8,128)(2,1)}, bf16[2048,1,128]{2,0,1:T(8,128)(2,1)}, u32[]{:S(2)}, u32[]{:S(2)}) collective-permute-start(bf16[2048,1,128]{2,0,1:T(8,128)(2,1)} %get-tuple-element.222), channel_id=1, source_target_pairs={{16,0},{32,16},{48,32},{64,48},{80,64},{96,80},{112,96},{17,1},{33... | collective-permute-start | bytes 1572872 | tf_op jit(solution)/shard_map/ppermute | solution.py:24
  41.3 72.4 %collective-permute-start.1 = (bf16[2048,1,128]{2,0,1:T(8,128)(2,1)}, bf16[2048,1,128]{2,0,1:T(8,128)(2,1)}, u32[]{:S(2)}, u32[]{:S(2)}) collective-permute-start(bf16[2048,1,128]{2,0,1:T(8,128)(2,1)} %get-tuple-element.221), channel_id=1, source_target_pairs={{0,16},{16,32},{32,48},{48,64},{64,80},{80,96},{96,112},{1,17},{17... | collective-permute-start | bytes 1572872 | tf_op jit(solution)/shard_map/ppermute | solution.py:24
  47.6 107.9 %collective-permute-start.3 = (bf16[2048,1,128]{2,0,1:T(8,128)(2,1)}, bf16[2048,1,128]{2,0,1:T(8,128)(2,1)}, u32[]{:S(2)}, u32[]{:S(2)}) collective-permute-start(bf16[2048,1,128]{2,0,1:T(8,128)(2,1)} %get-tuple-element.221), channel_id=1, source_target_pairs={{16,0},{32,16},{48,32},{64,48},{80,64},{96,80},{112,96},{17,1},{33... | collective-permute-start | bytes 1572872 | tf_op jit(solution)/shard_map/ppermute | solution.py:24
  48.9 1.0 copy-start.2
  55.0 3.5 %copy-start.1 = (f32[256,2048,2]{1,0,2:T(8,128)S(1)}, f32[256,2048,2]{1,0,2:T(8,128)}, u32[]{:S(2)}) copy-start(f32[256,2048,2]{1,0,2:T(8,128)} %get-tuple-element.386) | copy-start | bytes 12582916 | tf_op jit(solution)/shard_map/while
  62.8 3.5 %copy-start.1 = (f32[256,2048,2]{1,0,2:T(8,128)S(1)}, f32[256,2048,2]{1,0,2:T(8,128)}, u32[]{:S(2)}) copy-start(f32[256,2048,2]{1,0,2:T(8,128)} %get-tuple-element.386) | copy-start | bytes 12582916 | tf_op jit(solution)/shard_map/while
  70.6 3.5 %copy-start.1 = (f32[256,2048,2]{1,0,2:T(8,128)S(1)}, f32[256,2048,2]{1,0,2:T(8,128)}, u32[]{:S(2)}) copy-start(f32[256,2048,2]{1,0,2:T(8,128)} %get-tuple-element.386) | copy-start | bytes 12582916 | tf_op jit(solution)/shard_map/while
  78.4 3.5 %copy-start.1 = (f32[256,2048,2]{1,0,2:T(8,128)S(1)}, f32[256,2048,2]{1,0,2:T(8,128)}, u32[]{:S(2)}) copy-start(f32[256,2048,2]{1,0,2:T(8,128)} %get-tuple-element.386) | copy-start | bytes 12582916 | tf_op jit(solution)/shard_map/while
  86.1 3.5 %copy-start.1 = (f32[256,2048,2]{1,0,2:T(8,128)S(1)}, f32[256,2048,2]{1,0,2:T(8,128)}, u32[]{:S(2)}) copy-start(f32[256,2048,2]{1,0,2:T(8,128)} %get-tuple-element.386) | copy-start | bytes 12582916 | tf_op jit(solution)/shard_map/while
  93.9 3.5 %copy-start.1 = (f32[256,2048,2]{1,0,2:T(8,128)S(1)}, f32[256,2048,2]{1,0,2:T(8,128)}, u32[]{:S(2)}) copy-start(f32[256,2048,2]{1,0,2:T(8,128)} %get-tuple-element.386) | copy-start | bytes 12582916 | tf_op jit(solution)/shard_map/while
  101.7 3.5 %copy-start.1 = (f32[256,2048,2]{1,0,2:T(8,128)S(1)}, f32[256,2048,2]{1,0,2:T(8,128)}, u32[]{:S(2)}) copy-start(f32[256,2048,2]{1,0,2:T(8,128)} %get-tuple-element.386) | copy-start | bytes 12582916 | tf_op jit(solution)/shard_map/while
  109.4 3.5 %copy-start.1 = (f32[256,2048,2]{1,0,2:T(8,128)S(1)}, f32[256,2048,2]{1,0,2:T(8,128)}, u32[]{:S(2)}) copy-start(f32[256,2048,2]{1,0,2:T(8,128)} %get-tuple-element.386) | copy-start | bytes 12582916 | tf_op jit(solution)/shard_map/while
where the time goes:
time: 246 us; the launch traced here: 244 us
  matrix products  122 us (50%)
  blocking collectives  43.2 us (18%)
  starting transfers between devices  26.4 us (11%)
  other arithmetic  22.9 us (9%)
  waiting for transfers between devices  14.5 us (6%)
  local copies, waits for them, and re-layouts  13.1 us (5%)
    dot_general x24, matrix products, one_block(): jnp.einsum('grqk,kgd->grqd', weights.astype(jnp.bfloat16), value_block, p...  69.2 us
    dot_general x24, matrix products, one_block(): jnp.einsum('qgrd,kgd->grqk', grouped, key_block, preferred_element_type=j...  53 us
    all_to_all x2, blocking collectives, exchange_in_order(): lax.all_to_all(parts, axes[k], split_axis=k, concat_axis=k, tiled=True)  43.2 us
    reduce_sum x24, other arithmetic, one_block(): total = total * factor + jnp.sum(weights, axis=-1)  19.6 us
    ppermute x4, starting transfers between devices, shifted(): return lax.ppermute(block, axis, route)  14.9 us
    all_to_all x1, waiting for transfers between devices, sent_together(): lax.all_to_all(both, axis, split_axis=split_dim, concat_axis=concat_dim,...  14.4 us
    all_to_all x1, starting transfers between devices, sent_together(): lax.all_to_all(both, axis, split_axis=split_dim, concat_axis=concat_dim,...  7.33 us
  transfers between devices with their start and end apart: 6, of which 1 were waited for; matrix products, arithmetic and copies ran while one was open for 44% of the time, Pallas kernels for 0%

commit v1 on v0

v1 whole, which is shorter than its diff:
```python
import jax
import jax.numpy as jnp
from jax import lax
from jax.experimental import pallas as pl
from jax.experimental.pallas import tpu as pltpu
from jax.sharding import PartitionSpec as P

QH = 32
KVH = 8
HD = 128
TOK = 128
RATIO = QH // KVH
ROWS = RATIO * TOK
HALF = 8 * TOK
SEG = 2 * HALF
KT = 256
SCALE = 1.4426950408889634 / HD**0.5
MESH = pl.DeviceIdType.MESH


def rotation(slot):
    turn = slot // 2
    return turn + (turn // 2) * (5 - 2 * turn), slot % 2


def mirrored(slot):
    turn = slot // 2
    return 2 * ((2 * turn) % 3 + 3 * (turn // 3)) + slot % 2


def kernel(
    q_hbm, k_hbm, v_hbm, o_hbm,
    q_buf, k_buf, v_buf, o_buf, s_buf, m_cur, m_run, acc,
    q_out, q_in, kv_out, kv_in, sib_out, sib_in, hop_out, hop_in, o_out, o_in,
):
    outer = lax.axis_index("outer")
    inner = lax.axis_index("inner")
    z_hi = outer % 2
    z_lo = inner // 8
    y = (inner // 2) % 4
    core = inner % 2

    def peer(slot):
        dy, dz = rotation(slot)
        py = (y + dy) % 4
        pz = (z_lo + dz) % 2
        head = ((pz + z_hi) % 2) * 4 + py
        return (outer, pz * 8 + py * 2 + core), head

    def columns(head, width):
        return pl.ds(pl.multiple_of(head * width, width), width)

    my_head = ((z_lo + z_hi) % 2) * 4 + y
    sibling = (outer, inner + 1 - 2 * core)
    across = (1 - z_lo) * 8 + y * 2 + core
    near = (outer + 1 - 2 * z_hi, across)
    far_outer = outer - 1 + 2 * z_hi
    far = (far_outer, across)
    has_far = jnp.logical_and(far_outer >= 0, far_outer < 8)
    no_far = jnp.logical_not(has_far)

    barrier = pltpu.get_barrier_semaphore()

    def greet(device):
        pl.semaphore_signal(barrier, inc=1, device_id=device, device_id_type=MESH)

    for slot in range(1, 8):
        greet(peer(slot)[0])
    greet(sibling)
    greet(near)

    @pl.when(has_far)
    def _():
        greet(far)
        pl.semaphore_wait(barrier, 10)

    @pl.when(no_far)
    def _():
        pl.semaphore_wait(barrier, 9)

    def remote(src, dst, send, recv, device):
        return pltpu.make_async_remote_copy(
            src_ref=src, dst_ref=dst, send_sem=send, recv_sem=recv,
            device_id=device, device_id_type=MESH,
        )

    def kv_copy(slot, which):
        device, head = peer(slot)
        back = mirrored(slot)
        hbm, buf = ((k_hbm, k_buf), (v_hbm, v_buf))[which]
        return remote(
            hbm.at[:, columns(head, HD)],
            buf.at[0, 0, pl.ds(back * TOK, TOK), :],
            kv_out.at[which, slot], kv_in.at[which, back], device,
        )

    def q_copy(slot):
        device, head = peer(slot)
        back = mirrored(slot)
        return remote(
            q_hbm.at[:, columns(head, RATIO * HD)],
            q_buf.at[back], q_out.at[slot], q_in.at[back], device,
        )

    def own_kv(which):
        hbm, buf = ((k_hbm, k_buf), (v_hbm, v_buf))[which]
        return pltpu.make_async_copy(
            hbm.at[:, columns(my_head, HD)],
            buf.at[0, 0, pl.ds(0, TOK), :], kv_in.at[which, 0],
        )

    own_q = pltpu.make_async_copy(
        q_hbm.at[:, columns(my_head, RATIO * HD)], q_buf.at[0], q_in.at[0]
    )

    for which in range(2):
        own_kv(which).start()
    for slot in range(1, 8):
        for which in range(2):
            kv_copy(slot, which).start()
    own_q.start()
    for slot in range(1, 8):
        q_copy(slot).start()

    def to_sibling(seg, which):
        buf = (k_buf, v_buf)[which]
        return remote(
            buf.at[seg, 0], buf.at[seg, 1],
            sib_out.at[seg, which], sib_in.at[seg, which], sibling,
        )

    def hop(seg, which):
        buf = (k_buf, v_buf)[which]
        return remote(
            buf.at[0, 0], buf.at[seg, 0],
            hop_out.at[seg - 1, which], hop_in.at[seg - 1, which],
            near if seg == 1 else far,
        )

    for which in range(2):
        own_kv(which).wait()
        for slot in range(1, 8):
            kv_copy(slot, which).wait_recv()
        to_sibling(0, which).start()
        hop(1, which).start()
    own_q.wait()

    def wait_q(slot):
        remote(
            q_hbm.at[:, columns(0, RATIO * HD)],
            q_buf.at[slot], q_out.at[slot], q_in.at[slot], sibling,
        ).wait_recv()

    def score(b, seg, side):
        q = jnp.concatenate(
            [q_buf[b, :, h * HD : (h + 1) * HD] for h in range(RATIO)], axis=0
        )
        for kt in range(SEG // KT):
            half, at = divmod(kt * KT, HALF)
            s_buf[side, :, kt * KT : (kt + 1) * KT] = lax.dot_general(
                q, k_buf[seg, half, at : at + KT, :],
                (((1,), (1,)), ((), ())), preferred_element_type=jnp.float32,
            )
        for h in range(RATIO):
            r = slice(h * TOK, (h + 1) * TOK)
            top = s_buf[side, r, 0:HD]
            for j in range(1, SEG // HD):
                top = jnp.maximum(top, s_buf[side, r, j * HD : (j + 1) * HD])
            top = jnp.broadcast_to(jnp.max(top, axis=1, keepdims=True), (TOK, HD))
            if seg:
                top = jnp.maximum(top, m_run[b, r, :])
            m_cur[side, r, :] = top

    def mix(b, seg, side):
        m = m_cur[side]
        update = None
        for kt in range(SEG // KT):
            half, at = divmod(kt * KT, HALF)
            p = jnp.concatenate(
                [
                    jnp.exp2((s_buf[side, :, c : c + HD] - m) * SCALE).astype(jnp.bfloat16)
                    for c in range(kt * KT, (kt + 1) * KT, HD)
                ],
                axis=1,
            )
            wide = jnp.concatenate(
                [v_buf[seg, half, at : at + KT, :], jnp.ones((KT, HD), jnp.bfloat16)], axis=1
            )
            part = jnp.dot(p, wide, preferred_element_type=jnp.float32)
            update = part if update is None else update + part
        if seg:
            factor = jnp.exp2((m_run[b] - m) * SCALE)
            update = acc[b] * jnp.concatenate([factor, factor], axis=1) + update
        if seg < 2:
            m_run[b] = m
            acc[b] = update
        else:
            finish(b, update)

    def finish(b, total):
        mixed = (total[:, :HD] / total[:, HD:]).astype(jnp.bfloat16)
        for h in range(RATIO):
            o_buf[b, :, h * HD : (h + 1) * HD] = mixed[h * TOK : (h + 1) * TOK, :]

    def give(b):
        device, head = peer(b)
        return remote(
            o_buf.at[b], o_hbm.at[:, columns(my_head, RATIO * HD)],
            o_out.at[b], o_in.at[mirrored(b)], device,
        )

    own_o = pltpu.make_async_copy(
        o_buf.at[0], o_hbm.at[:, columns(my_head, RATIO * HD)], o_in.at[0]
    )

    def send_out(b):
        @pl.when(b == 0)
        def _():
            own_o.start()

        @pl.when(b > 0)
        def _():
            give(b).start()

    for which in range(2):
        to_sibling(0, which).wait_recv()

    def phase(seg, before_last):
        score(0, seg, 0)

        def body(i, carry):
            b = 2 * i
            if seg == 0:
                wait_q(b + 1)
            if before_last is not None:
                pl.when(i == 3)(before_last)
            score(b + 1, seg, 1)
            mix(b, seg, 0)
            if seg == 0:

                @pl.when(i < 3)
                def _():
                    wait_q(b + 2)

            if seg == 2:
                send_out(b)
            score(jnp.minimum(b + 2, 7), seg, 0)
            mix(b + 1, seg, 1)
            if seg == 2:
                send_out(b + 1)
            return carry

        lax.fori_loop(0, 4, body, 0)

    def near_arrives():
        for which in range(2):
            hop(1, which).wait_recv()
            to_sibling(1, which).start()

        @pl.when(has_far)
        def _():
            for which in range(2):
                hop(2, which).start()

    def far_arrives():
        @pl.when(has_far)
        def _():
            for which in range(2):
                hop(2, which).wait_recv()
                to_sibling(2, which).start()

    phase(0, near_arrives)
    for which in range(2):
        to_sibling(1, which).wait_recv()
    phase(1, far_arrives)

    @pl.when(has_far)
    def _():
        for which in range(2):
            to_sibling(2, which).wait_recv()
        phase(2, None)

    @pl.when(no_far)
    def _():
        def body(b, carry):
            finish(b, acc[b])
            send_out(b)
            return carry

        lax.fori_loop(0, 8, body, 0)

    for slot in range(1, 8):
        for which in range(2):
            kv_copy(slot, which).wait_send()
        q_copy(slot).wait_send()
    for which in range(2):
        to_sibling(0, which).wait_send()
        to_sibling(1, which).wait_send()
        hop(1, which).wait_send()

    @pl.when(has_far)
    def _():
        for which in range(2):
            to_sibling(2, which).wait_send()
            hop(2, which).wait_send()

    own_o.wait()
    for slot in range(1, 8):
        device, head = peer(slot)
        give(slot).wait_send()
        remote(
            o_buf.at[slot], o_hbm.at[:, columns(head, RATIO * HD)],
            o_out.at[slot], o_in.at[slot], device,
        ).wait_recv()


def attention(queries, keys, values):
    dma = pltpu.SemaphoreType.DMA
    return pl.pallas_call(
        kernel,
        out_shape=jax.ShapeDtypeStruct(queries.shape, jnp.bfloat16),
        in_specs=[pl.BlockSpec(memory_space=pl.ANY)] * 3,
        out_specs=pl.BlockSpec(memory_space=pl.ANY),
        scratch_shapes=[
            pltpu.VMEM((8, TOK, RATIO * HD), jnp.bfloat16),
            pltpu.VMEM((3, 2, HALF, HD), jnp.bfloat16),
            pltpu.VMEM((3, 2, HALF, HD), jnp.bfloat16),
            pltpu.VMEM((8, TOK, RATIO * HD), jnp.bfloat16),
            pltpu.VMEM((2, ROWS, SEG), jnp.float32),
            pltpu.VMEM((2, ROWS, HD), jnp.float32),
            pltpu.VMEM((8, ROWS, HD), jnp.float32),
            pltpu.VMEM((8, ROWS, 2 * HD), jnp.float32),
            dma((8,)), dma((8,)),
            dma((2, 8)), dma((2, 8)),
            dma((3, 2)), dma((3, 2)),
            dma((2, 2)), dma((2, 2)),
            dma((8,)), dma((8,)),
        ],
        compiler_params=pltpu.CompilerParams(
            collective_id=0, has_side_effects=True, vmem_limit_bytes=58 * 2**20
        ),
        name="window_attention",
    )(queries, keys, values)


def solution(mesh):
    spec = P(("outer", "inner"), None)
    return jax.shard_map(
        attention, mesh=mesh, in_specs=(spec, spec, spec), out_specs=spec, check_vma=False
    )
```

time: 246 us -> 69 us (0.28)
  the two profiles are of different devices: /device:TPU:1 before, /device:TPU:14 now
where the time goes in v1:
time: 69 us; the launch traced here: 68.9 us
  Pallas kernels  66.6 us (97%)
  local copies, waits for them, and re-layouts  2.29 us (3%)
    pallas_call x1, Pallas kernels, attention(): pl.pallas_call(kernel, out_shape=jax.ShapeDtypeStruct(queries.shape, jnp....  66.6 us
    unnamed x1, local copies, waits for them, and re-layouts  2.29 us

profile of v1, /device:TPU:14, one launch (start us, length us, event | category | flops | bytes accessed | tf_op | source)
XLA Modules:
  0.0 68.9 jit_solution(11741507201658657403)
XLA Ops:
  0.0 66.6 %window_attention.1 = bf16[128,4096]{1,0:T(8,128)(2,1)} custom-call(bf16[128,4096]{1,0:T(8,128)(2,1)} %q_hbm.1, bf16[128,1024]{1,0:T(8,128)(2,1)} %k_hbm.1, bf16[128,1024]{1,0:T(8,128)(2,1)} %v_hbm.1), custom_call_target="tpu_custom_call" | custom-call | tf_op jit(solution)/shard_map/window_attention/pallas_call | solution.py:319
  66.6 2.3 %copy.5 = bf16[128,4096]{1,0:T(8,128)(2,1)} copy(bf16[128,4096]{1,0:T(8,128)(2,1)} %window_attention.1) | data formatting | bytes 2097152

commit v2 on v1

v2 whole, which is shorter than its diff:
```python
import jax
import jax.numpy as jnp
from jax import lax
from jax.experimental import pallas as pl
from jax.experimental.pallas import tpu as pltpu
from jax.sharding import PartitionSpec as P

QH = 32
KVH = 8
HD = 128
TOK = 128
RATIO = QH // KVH
ROWS = RATIO * TOK
HALF = 8 * TOK
SEG = 2 * HALF
KT = 256
SCALE = 1.4426950408889634 / HD**0.5
MESH = pl.DeviceIdType.MESH


STEPS = ((0, 0), (1, 0), (3, 0), (0, 1), (1, 1), (3, 1), (2, 0), (2, 1))
BACK = tuple(STEPS.index(((4 - dy) % 4, dz)) for dy, dz in STEPS)
CHUNKS = 4
CHUNK = HALF // CHUNKS


def kernel(
    q_hbm, k_hbm, v_hbm, o_hbm,
    q_buf, k_buf, v_buf, o_buf, s_buf, m_cur, m_run, acc,
    q_out, q_in, kv_out, kv_in, own_out, own_in, hop_out, hop_in,
    next_out, next_in, relay_out, relay_in, last_out, last_in, o_out, o_in,
):
    outer = lax.axis_index("outer")
    inner = lax.axis_index("inner")
    z_hi = outer % 2
    z_lo = inner // 8
    y = (inner // 2) % 4
    core = inner % 2
    kv = ((k_hbm, k_buf), (v_hbm, v_buf))

    def peer(slot):
        dy, dz = STEPS[slot]
        py = (y + dy) % 4
        pz = (z_lo + dz) % 2
        head = ((pz + z_hi) % 2) * 4 + py
        return (outer, pz * 8 + py * 2 + core), head

    def columns(head, width):
        return pl.ds(pl.multiple_of(head * width, width), width)

    my_head = ((z_lo + z_hi) % 2) * 4 + y
    sibling = (outer, inner + 1 - 2 * core)
    near = (outer + 1 - 2 * z_hi, (1 - z_lo) * 8 + y * 2 + core)
    onward_outer = outer + 2 - 4 * z_hi
    source_outer = outer - 2 + 4 * z_hi
    onward = (onward_outer, inner)
    source = (source_outer, inner)
    has_onward = jnp.logical_and(onward_outer >= 0, onward_outer < 8)
    has_far = jnp.logical_and(source_outer >= 0, source_outer < 8)
    no_far = jnp.logical_not(has_far)

    barrier = pltpu.get_barrier_semaphore()

    def greet(device):
        pl.semaphore_signal(barrier, inc=1, device_id=device, device_id_type=MESH)

    for slot in range(1, 8):
        greet(peer(slot)[0])
    greet(sibling)
    greet(near)

    @pl.when(has_onward)
    def _():
        greet(onward)

    @pl.when(has_far)
    def _():
        greet(source)

    inland = jnp.logical_and(has_onward, has_far)

    @pl.when(inland)
    def _():
        pl.semaphore_wait(barrier, 11)

    @pl.when(jnp.logical_not(inland))
    def _():
        pl.semaphore_wait(barrier, 10)

    def remote(src, dst, send, recv, device):
        return pltpu.make_async_remote_copy(
            src_ref=src, dst_ref=dst, send_sem=send, recv_sem=recv,
            device_id=device, device_id_type=MESH,
        )

    def kv_copy(slot, which):
        device, head = peer(slot)
        hbm, buf = kv[which]
        back = BACK[slot]
        return remote(
            hbm.at[:, columns(head, HD)],
            buf.at[0, 0, pl.ds(back * TOK, TOK), :],
            kv_out.at[which, slot], kv_in.at[which, back], device,
        )

    def q_copy(slot):
        device, head = peer(slot)
        back = BACK[slot]
        return remote(
            q_hbm.at[:, columns(head, RATIO * HD)],
            q_buf.at[back], q_out.at[slot], q_in.at[back], device,
        )

    def own_kv(which):
        hbm, buf = kv[which]
        return pltpu.make_async_copy(
            hbm.at[:, columns(my_head, HD)],
            buf.at[0, 0, pl.ds(0, TOK), :], kv_in.at[which, 0],
        )

    own_q = pltpu.make_async_copy(
        q_hbm.at[:, columns(my_head, RATIO * HD)], q_buf.at[0], q_in.at[0]
    )

    for which in range(2):
        own_kv(which).start()
    for slot in range(1, 8):
        for which in range(2):
            kv_copy(slot, which).start()
    own_q.start()
    for slot in range(1, 8):
        q_copy(slot).start()

    def piece(buf, seg, half, chunk):
        at = pl.multiple_of(chunk * CHUNK, CHUNK)
        return buf.at[seg, half, pl.ds(at, CHUNK), :]

    def own_to_sibling(which, chunk):
        buf = kv[which][1]
        return remote(
            piece(buf, 0, 0, chunk), piece(buf, 0, 1, chunk),
            own_out.at[which, chunk], own_in.at[which, chunk], sibling,
        )

    def hop(which, chunk):
        buf = kv[which][1]
        return remote(
            piece(buf, 0, 0, chunk), piece(buf, 1, 0, chunk),
            hop_out.at[which, chunk], hop_in.at[which, chunk], near,
        )

    def near_to_sibling(which, chunk):
        buf = kv[which][1]
        return remote(
            piece(buf, 1, 0, chunk), piece(buf, 1, 1, chunk),
            next_out.at[which, chunk], next_in.at[which, chunk], sibling,
        )

    def relay(which, chunk):
        buf = kv[which][1]
        return remote(
            piece(buf, 1, 0, chunk), piece(buf, 2, 0, chunk),
            relay_out.at[which, chunk], relay_in.at[which, chunk], onward,
        )

    def far_to_sibling(which):
        buf = kv[which][1]
        return remote(
            buf.at[2, 0], buf.at[2, 1], last_out.at[which], last_in.at[which], sibling
        )

    m_run[...] = jnp.full(m_run.shape, -jnp.inf, jnp.float32)
    for chunk in range(CHUNKS):
        for which in range(2):
            for slot in (2 * chunk, 2 * chunk + 1):
                if slot == 0:
                    own_kv(which).wait()
                else:
                    kv_copy(BACK[slot], which).wait_recv()
            own_to_sibling(which, chunk).start()
            hop(which, chunk).start()
    own_q.wait()

    def wait_q(slot):
        remote(
            q_hbm.at[:, columns(0, RATIO * HD)],
            q_buf.at[slot], q_out.at[slot], q_in.at[slot], sibling,
        ).wait_recv()

    def score(b, seg, side, floor=None, between=None):
        q = jnp.concatenate(
            [q_buf[b, :, h * HD : (h + 1) * HD] for h in range(RATIO)], axis=0
        )
        for kt in range(SEG // KT):
            half, at = divmod(kt * KT, HALF)
            if between is not None and kt * KT == HALF:
                between()
            s_buf[side, :, kt * KT : (kt + 1) * KT] = lax.dot_general(
                q, k_buf[seg, half, at : at + KT, :],
                (((1,), (1,)), ((), ())), preferred_element_type=jnp.float32,
            )
        for h in range(RATIO):
            r = slice(h * TOK, (h + 1) * TOK)
            top = s_buf[side, r, 0:HD]
            for j in range(1, SEG // HD):
                top = jnp.maximum(top, s_buf[side, r, j * HD : (j + 1) * HD])
            top = jnp.broadcast_to(jnp.max(top, axis=1, keepdims=True), (TOK, HD))
            if floor is not None:
                top = jnp.maximum(top, floor[r, :])
            m_cur[side, r, :] = top

    def mix(b, seg, side, last=False):
        m = m_cur[side]
        update = None
        for kt in range(SEG // KT):
            half, at = divmod(kt * KT, HALF)
            p = jnp.concatenate(
                [
                    jnp.exp2((s_buf[side, :, c : c + HD] - m) * SCALE).astype(jnp.bfloat16)
                    for c in range(kt * KT, (kt + 1) * KT, HD)
                ],
                axis=1,
            )
            wide = jnp.concatenate(
                [v_buf[seg, half, at : at + KT, :], jnp.ones((KT, HD), jnp.bfloat16)], axis=1
            )
            part = jnp.dot(p, wide, preferred_element_type=jnp.float32)
            update = part if update is None else update + part
        if seg:
            factor = jnp.exp2((m_run[b] - m) * SCALE)
            update = acc[b] * jnp.concatenate([factor, factor], axis=1) + update
        if last:
            finish(b, update)
        else:
            m_run[b] = m
            acc[b] = update

    def finish(b, total):
        mixed = (total[:, :HD] / total[:, HD:]).astype(jnp.bfloat16)
        for h in range(RATIO):
            o_buf[b, :, h * HD : (h + 1) * HD] = mixed[h * TOK : (h + 1) * TOK, :]

    def give(slot):
        device, head = peer(slot)
        return remote(
            o_buf.at[slot], o_hbm.at[:, columns(my_head, RATIO * HD)],
            o_out.at[slot], o_in.at[BACK[slot]], device,
        )

    own_o = pltpu.make_async_copy(
        o_buf.at[0], o_hbm.at[:, columns(my_head, RATIO * HD)], o_in.at[0]
    )

    def send_out(b):
        for slot in range(1, 8):
            pl.when(b == slot)(give(slot).start)

    def own_arrives():
        for chunk in range(CHUNKS):
            for which in range(2):
                own_to_sibling(which, chunk).wait_recv()

    def near_arrives(chunk):
        for which in range(2):
            hop(which, chunk).wait_recv()
            near_to_sibling(which, chunk).start()

        @pl.when(has_onward)
        def _():
            for which in range(2):
                relay(which, chunk).start()

    def far_arrives():
        for which in range(2):
            for chunk in range(CHUNKS):
                relay(which, chunk).wait_recv()
            far_to_sibling(which).start()
        for which in range(2):
            far_to_sibling(which).wait_recv()

    score(0, 0, 0, None, own_arrives)

    def own_pair(i, carry):
        b = 2 * i
        wait_q(b + 1)

        @pl.when(i >= 1)
        def _():
            near_arrives(i - 1)

        score(b + 1, 0, 1)
        mix(b, 0, 0)

        wait_q(b + 2)
        score(b + 2, 0, 0)
        mix(b + 1, 0, 1)
        return carry

    lax.fori_loop(0, 3, own_pair, 0)
    wait_q(7)
    near_arrives(2)
    score(7, 0, 1)
    mix(6, 0, 0)
    near_arrives(3)
    for chunk in range(CHUNKS):
        for which in range(2):
            near_to_sibling(which, chunk).wait_recv()
    score(7, 1, 0, m_cur.at[1])
    mix(7, 0, 1)

    @pl.when(has_far)
    def _():
        far_arrives()

        def both(t, carry):
            b = 7 - t
            score(b, 2, 1, m_cur.at[0])
            mix(b, 1, 0)
            score(b - 1, 1, 0, m_run.at[b - 1])
            mix(b, 2, 1, True)
            send_out(b)
            return carry

        lax.fori_loop(0, 7, both, 0)
        score(0, 2, 1, m_cur.at[0])
        mix(0, 1, 0)
        mix(0, 2, 1, True)
        own_o.start()

    @pl.when(no_far)
    def _():
        def single(i, carry):
            b = 7 - 2 * i
            score(b - 1, 1, 1, m_run.at[b - 1])
            mix(b, 1, 0, True)
            send_out(b)
            score(b - 2, 1, 0, m_run.at[b - 2])
            mix(b - 1, 1, 1, True)
            send_out(b - 1)
            return carry

        lax.fori_loop(0, 3, single, 0)
        score(0, 1, 1, m_run.at[0])
        mix(1, 1, 0, True)
        give(1).start()
        mix(0, 1, 1, True)
        own_o.start()

    for slot in range(1, 8):
        for which in range(2):
            kv_copy(slot, which).wait_send()
        q_copy(slot).wait_send()
    for which in range(2):
        for chunk in range(CHUNKS):
            own_to_sibling(which, chunk).wait_send()
            hop(which, chunk).wait_send()
            near_to_sibling(which, chunk).wait_send()

    @pl.when(has_onward)
    def _():
        for which in range(2):
            for chunk in range(CHUNKS):
                relay(which, chunk).wait_send()

    @pl.when(has_far)
    def _():
        for which in range(2):
            far_to_sibling(which).wait_send()

    own_o.wait()
    for slot in range(1, 8):
        device, head = peer(slot)
        give(slot).wait_send()
        remote(
            o_buf.at[slot], o_hbm.at[:, columns(head, RATIO * HD)],
            o_out.at[slot], o_in.at[slot], device,
        ).wait_recv()


def attention(queries, keys, values):
    dma = pltpu.SemaphoreType.DMA
    return pl.pallas_call(
        kernel,
        out_shape=jax.ShapeDtypeStruct(queries.shape, jnp.bfloat16),
        in_specs=[pl.BlockSpec(memory_space=pl.ANY)] * 3,
        out_specs=pl.BlockSpec(memory_space=pl.ANY),
        scratch_shapes=[
            pltpu.VMEM((8, TOK, RATIO * HD), jnp.bfloat16),
            pltpu.VMEM((3, 2, HALF, HD), jnp.bfloat16),
            pltpu.VMEM((3, 2, HALF, HD), jnp.bfloat16),
            pltpu.VMEM((8, TOK, RATIO * HD), jnp.bfloat16),
            pltpu.VMEM((2, ROWS, SEG), jnp.float32),
            pltpu.VMEM((2, ROWS, HD), jnp.float32),
            pltpu.VMEM((8, ROWS, HD), jnp.float32),
            pltpu.VMEM((8, ROWS, 2 * HD), jnp.float32),
            dma((8,)), dma((8,)),
            dma((2, 8)), dma((2, 8)),
            dma((2, CHUNKS)), dma((2, CHUNKS)),
            dma((2, CHUNKS)), dma((2, CHUNKS)),
            dma((2, CHUNKS)), dma((2, CHUNKS)),
            dma((2, CHUNKS)), dma((2, CHUNKS)),
            dma((2,)), dma((2,)),
            dma((8,)), dma((8,)),
        ],
        compiler_params=pltpu.CompilerParams(
            collective_id=0, has_side_effects=True, vmem_limit_bytes=58 * 2**20
        ),
        name="window_attention",
    )(queries, keys, values)


def solution(mesh):
    spec = P(("outer", "inner"), None)
    return jax.shard_map(
        attention, mesh=mesh, in_specs=(spec, spec, spec), out_specs=spec, check_vma=False
    )
```

time: 69 us -> 62.1 us (0.900)
  the two profiles are of different devices: /device:TPU:14 before, /device:TPU:39 now
where the time goes in v2:
time: 62.1 us; the launch traced here: 61.9 us
  Pallas kernels  59.6 us (96%)
  local copies, waits for them, and re-layouts  2.29 us (4%)
    pallas_call x1, Pallas kernels, attention(): pl.pallas_call(kernel, out_shape=jax.ShapeDtypeStruct(queries.shape, jnp....  59.6 us
    unnamed x1, local copies, waits for them, and re-layouts  2.29 us

profile of v2, /device:TPU:39, one launch (start us, length us, event | category | flops | bytes accessed | tf_op | source)
XLA Modules:
  0.0 61.9 jit_solution(3025554654214503139)
XLA Ops:
  0.0 59.6 %window_attention.1 = bf16[128,4096]{1,0:T(8,128)(2,1)} custom-call(bf16[128,4096]{1,0:T(8,128)(2,1)} %q_hbm.1, bf16[128,1024]{1,0:T(8,128)(2,1)} %k_hbm.1, bf16[128,1024]{1,0:T(8,128)(2,1)} %v_hbm.1), custom_call_target="tpu_custom_call" | custom-call | tf_op jit(solution)/shard_map/window_attention/pallas_call | solution.py:382
  59.6 2.3 %copy.5 = bf16[128,4096]{1,0:T(8,128)(2,1)} copy(bf16[128,4096]{1,0:T(8,128)(2,1)} %window_attention.1) | data formatting | bytes 2097152

commit v3 on v2

--- a/solution.py
+++ b/solution.py
@@ -275,8 +275,6 @@
             for chunk in range(CHUNKS):
                 relay(which, chunk).wait_recv()
             far_to_sibling(which).start()
-        for which in range(2):
-            far_to_sibling(which).wait_recv()
 
     score(0, 0, 0, None, own_arrives)
 
@@ -310,18 +308,44 @@
 
     @pl.when(has_far)
     def _():
-        far_arrives()
-
-        def both(t, carry):
-            b = 7 - t
-            score(b, 2, 1, m_cur.at[0])
+        def near_pair(i, carry):
+            b = 7 - 2 * i
+
+            @pl.when(i == 2)
+            def _():
+                far_arrives()
+
+            score(b - 1, 1, 1, m_run.at[b - 1])
             mix(b, 1, 0)
-            score(b - 1, 1, 0, m_run.at[b - 1])
-            mix(b, 2, 1, True)
+
+            @pl.when(i == 2)
+            def _():
+                for which in range(2):
+                    far_to_sibling(which).wait_recv()
+
+            then = i // 2
+            score(b - 2 + 6 * then, 1 + then, 0, m_run.at[b - 2 + 6 * then])
+            mix(b - 1, 1, 1)
+            return carry
+
+        lax.fori_loop(0, 3, near_pair, 0)
+
+        def far_pair(i, carry):
+            b = 7 - 2 * i
+            score(b - 1, 2, 1, m_run.at[b - 1])
+            mix(b, 2, 0, True)
             send_out(b)
+            score(b - 2, 2 - i // 2, 0, m_run.at[b - 2])
+            mix(b - 1, 2, 1, True)
+            send_out(b - 1)
             return carry
 
-        lax.fori_loop(0, 7, both, 0)
+        lax.fori_loop(0, 3, far_pair, 0)
+        score(1, 2, 1, m_cur.at[0])
+        mix(1, 1, 0)
+        score(0, 1, 0, m_run.at[0])
+        mix(1, 2, 1, True)
+        give(1).start()
         score(0, 2, 1, m_cur.at[0])
         mix(0, 1, 0)
         mix(0, 2, 1, True)
@@ -403,10 +427,10 @@
             dma((8,)), dma((8,)),
         ],
         compiler_params=pltpu.CompilerParams(
-            collective_id=0, has_side_effects=True, vmem_limit_bytes=58 * 2**20
+            collective_id=0, has_side_effects=True, vmem_limit_bytes=30 * 2**20
         ),
         name="window_attention",
-    )(queries, keys, values)
+    )(*(pltpu.with_memory_space_constraint(a, pltpu.HBM) for a in (queries, keys, values)))
 
 
 def solution(mesh):

time: 62.1 us -> 59.1 us (0.952)
  Pallas kernels: 59.6 us -> 57.6 us
  local copies, waits for them, and re-layouts: 2.29 us -> 0.97 us
    pallas_call x1, Pallas kernels: 59.6 us -> 57.6 us  [attention(): pl.pallas_call(kernel, out_shape=jax.ShapeDtypeStruct(queries.shape, jnp....]
    unnamed x1, local copies, waits for them, and re-layouts: 2.29 us -> 0.97 us
where the time goes in v3:
time: 59.1 us; the launch traced here: 58.6 us
  Pallas kernels  57.6 us (97%)
  local copies, waits for them, and re-layouts  0.97 us (2%)
    pallas_call x1, Pallas kernels, attention(): pl.pallas_call(kernel, out_shape=jax.ShapeDtypeStruct(queries.shape, jnp....  57.6 us

profile of v3, /device:TPU:39, one launch (start us, length us, event | category | flops | bytes accessed | tf_op | source)
XLA Modules:
  0.0 58.6 jit_solution(14570841514610198338)
XLA Ops:
  0.0 57.6 %window_attention.1 = bf16[128,4096]{1,0:T(8,128)(2,1)S(1)} custom-call(bf16[128,4096]{1,0:T(8,128)(2,1)} %q_hbm.1, bf16[128,1024]{1,0:T(8,128)(2,1)} %k_hbm.1, bf16[128,1024]{1,0:T(8,128)(2,1)} %v_hbm.1), custom_call_target="tpu_custom_call" | custom-call | tf_op jit(solution)/shard_map/window_attention/pallas_call | solution.py:406
  57.6 1.0 %copy.5 = bf16[128,4096]{1,0:T(8,128)(2,1)} copy(bf16[128,4096]{1,0:T(8,128)(2,1)S(1)} %window_attention.1) | data formatting | bytes 2097152

commit v4 on v3

--- a/solution.py
+++ b/solution.py
@@ -297,9 +297,9 @@
     lax.fori_loop(0, 3, own_pair, 0)
     wait_q(7)
     near_arrives(2)
+    near_arrives(3)
     score(7, 0, 1)
     mix(6, 0, 0)
-    near_arrives(3)
     for chunk in range(CHUNKS):
         for which in range(2):
             near_to_sibling(which, chunk).wait_recv()
@@ -311,12 +311,9 @@
         def near_pair(i, carry):
             b = 7 - 2 * i
 
-            @pl.when(i == 2)
-            def _():
-                far_arrives()
-
             score(b - 1, 1, 1, m_run.at[b - 1])
             mix(b, 1, 0)
+            pl.when(i == 1)(far_arrives)
 
             @pl.when(i == 2)
             def _():

time: 59.1 us -> 57.9 us (0.980)
  Pallas kernels: 57.6 us -> 56.5 us
    pallas_call x1, Pallas kernels: 57.6 us -> 56.5 us  [attention(): pl.pallas_call(kernel, out_shape=jax.ShapeDtypeStruct(queries.shape, jnp....]
where the time goes in v4:
time: 57.9 us; the launch traced here: 57.5 us
  Pallas kernels  56.5 us (98%)
  local copies, waits for them, and re-layouts  0.97 us (2%)
    pallas_call x1, Pallas kernels, attention(): pl.pallas_call(kernel, out_shape=jax.ShapeDtypeStruct(queries.shape, jnp....  56.5 us

profile of v4, /device:TPU:39, one launch (start us, length us, event | category | flops | bytes accessed | tf_op | source)
XLA Modules:
  0.0 57.5 jit_solution(7718387691005135202)
XLA Ops:
  0.0 56.5 %window_attention.1 = bf16[128,4096]{1,0:T(8,128)(2,1)S(1)} custom-call(bf16[128,4096]{1,0:T(8,128)(2,1)} %q_hbm.1, bf16[128,1024]{1,0:T(8,128)(2,1)} %k_hbm.1, bf16[128,1024]{1,0:T(8,128)(2,1)} %v_hbm.1), custom_call_target="tpu_custom_call" | custom-call | tf_op jit(solution)/shard_map/window_attention/pallas_call | solution.py:403
  56.5 1.0 %copy.5 = bf16[128,4096]{1,0:T(8,128)(2,1)} copy(bf16[128,4096]{1,0:T(8,128)(2,1)S(1)} %window_attention.1) | data formatting | bytes 2097152
